TPU v7x, 256 devices: a whole 4x4x8 slice. The times are simulated.
256 devices in a mesh: gx: 4 (over x_lo, core), gy: 8 (over z), gz: 8 (over x_hi, y).
Axes of the slice: x: 4 (x_hi: 2, x_lo: 2; x = x_hi * 2 + x_lo), y: 4, z: 8, core: 2. Of those that a mesh axis runs over, the one named last changes fastest.
Arguments:
- fractions: float32 [4, 8, 8, 3, 256], P('gx', 'gy', 'gz'), may hold values from 0 to 1
- velocity: float32 [4, 8, 8, 3, 256], P('gx', 'gy', 'gz'), may hold values from -30 to 30
- charge: float32 [4, 8, 8, 256], P('gx', 'gy', 'gz'), may hold values from -1.5 to 1.5
- drude_charge: float32 [4, 8, 8, 256], P('gx', 'gy', 'gz'), may hold values from -2.2 to -0.8
- screening: float32 [4, 8, 8, 256], P('gx', 'gy', 'gz'), may hold values from 0.2 to 2
- labels: int32 [4, 8, 8, 256], P('gx', 'gy', 'gz'), may hold values from 0 to 255
- masses: float32 [4, 8, 8, 256], P('gx', 'gy', 'gz'), may hold values from 4 to 32
- counts: int32 [4, 8, 8], P('gx', 'gy', 'gz'), may hold values from 128 to 256, as said below
- leaving: int32 [4, 8, 8, 6, 16], P('gx', 'gy', 'gz'), may hold values from -1 to 255, as said below
Outputs:
- staying: float32 [4, 8, 8, 9, 256], P('gx', 'gy', 'gz')
- arrivals: float32 [4, 8, 8, 14, 96], P('gx', 'gy', 'gz')
Inputs may be any that keep to these rules, and one draw needn't show every extreme that they name: `counts`: at least one box holds 256 atoms. `leaving`: entries name distinct live slots of their box, or are -1; in every box some face has all 16 entries used.
All inputs are finite; a program needn't handle non-finite values.
Results may differ from a plain program's by a relative error of at most 0.0003.
Values sent between devices are 32-bit elements; how exact they have to be, the bound alone decides.
A program may use at most 64 MiB of HBM per device.

v0:
```python
import functools
import math

import jax
import jax.numpy as jnp
from jax import lax
from jax.experimental import pallas as pl
from jax.experimental.pallas import tpu as pltpu
from jax.sharding import PartitionSpec as P

SLOTS = 256
MOVE = 16
ITERS = 3
CUTOFF = 12.0
DRUDE_GAIN = 0.3320636
KICK = 0.002 * 418.4 * 332.0636
TIMESTEP = 0.002
UNITS = ((1, 0, 0), (-1, 0, 0), (0, 1, 0), (0, -1, 0), (0, 0, 1), (0, 0, -1))
EDGE = max(12.0, (10.0 * SLOTS) ** (1.0 / 3.0))
SCALE = EDGE / CUTOFF
LN2 = math.log(2.0)
GROUPS = SLOTS // 8
CHUNK = 4
AXES = ("gx", "gy", "gz")
MESH = pl.DeviceIdType.MESH
HIGHEST = lax.Precision.HIGHEST


def code_offset(code):
    return lax.rem(code + 1, 3) - 1 if not isinstance(code, int) else (code + 1) % 3 - 1


def step_from(mine, sizes, step):
    return tuple(lax.rem(mine[a] + step[a] + sizes[a], sizes[a]) for a in range(3))


def columns(row):
    return jnp.transpose(jnp.broadcast_to(row, (128, SLOTS))).reshape(GROUPS, 8, 128)


def lane_sums(block):
    return jnp.sum(jnp.transpose(block.reshape(SLOTS, 128)), axis=0, keepdims=True)


def kernel(
    sizes,
    counts_ref,
    fractions_ref,
    velocity_ref,
    charge_ref,
    drude_ref,
    screening_ref,
    labels_ref,
    masses_ref,
    leaving_ref,
    staying_ref,
    arrivals_ref,
    statics,
    places,
    moments,
    target,
    coef_a,
    coef_b,
    totals,
    outbox,
    inbox,
    static_send,
    static_recv,
    moment_send,
    moment_recv,
    out_send,
    out_recv,
):
    mine = tuple(lax.axis_index(axis) for axis in AXES)
    steps = [(code_offset(k % 3), code_offset(k // 3 % 3), code_offset(k // 9)) for k in range(27)]
    peers = [step_from(mine, sizes, step) for step in steps]
    mirror = [(3 - k % 3) % 3 + 3 * ((3 - k // 3 % 3) % 3) + 9 * ((3 - k // 9) % 3) for k in range(27)]

    barrier = pltpu.get_barrier_semaphore()
    for k in range(26, 0, -1):
        pl.semaphore_signal(barrier, inc=1, device_id=peers[k], device_id_type=MESH)

    count = counts_ref[0, 0, 0]
    slots = lax.broadcasted_iota(jnp.int32, (1, SLOTS), 1)
    live = slots < count
    fractions = fractions_ref[0, 0, 0]
    charge = jnp.where(live, charge_ref[0, 0], 0.0)
    drude = jnp.where(live, drude_ref[0, 0], -1.0)
    screening = screening_ref[0, 0]
    label = labels_ref[0, 0].astype(jnp.float32)
    place = (fractions - 0.5) * SCALE
    root = math.sqrt(0.5 * CUTOFF**3 / LN2) * lax.rsqrt(DRUDE_GAIN * drude * drude)
    statics[0, 0:3] = place
    statics[0, 3:4] = charge * (1.0 / CUTOFF**2)
    statics[0, 4:5] = root
    statics[0, 5:6] = screening
    statics[0, 6:7] = label
    statics[0, 7:8] = jnp.zeros((1, SLOTS), jnp.float32)
    places[0, 0:3] = place
    for at, row in enumerate((place[0:1], place[1:2], place[2:3], -root, screening, label)):
        target[at] = columns(row)

    pl.semaphore_wait(barrier, 26)

    def static_copy(k, slot, device):
        return pltpu.make_async_remote_copy(
            src_ref=statics.at[0],
            dst_ref=statics.at[slot],
            send_sem=static_send.at[k],
            recv_sem=static_recv.at[slot],
            device_id=device,
            device_id_type=MESH,
        )

    def moment_copy(turn, k, slot, device):
        return pltpu.make_async_remote_copy(
            src_ref=moments.at[turn, 0],
            dst_ref=moments.at[turn, slot],
            send_sem=moment_send.at[turn, k],
            recv_sem=moment_recv.at[turn, slot],
            device_id=device,
            device_id_type=MESH,
        )

    for k in range(26, 0, -1):
        static_copy(k, mirror[k], peers[k]).start()

    def spread(row):
        return jnp.broadcast_to(row, (8, 128))

    def geometry(k, own):
        for half in range(2):
            lanes = pl.ds(half * 128, 128)
            source = [spread(places[k, d : d + 1, lanes]) for d in range(3)]
            source += [spread(statics[k, d : d + 1, lanes]) for d in range(3, 7)]

            def chunk(c, carry, half=half, lanes=lanes, source=source):
                at = pl.ds(c * CHUNK, CHUNK)
                deltas = [target[d, at] - source[d] for d in range(3)]
                dist_sq = deltas[0] * deltas[0] + deltas[1] * deltas[1] + deltas[2] * deltas[2]
                if own:
                    rows = c * (CHUNK * 8) + lax.broadcasted_iota(jnp.int32, (CHUNK, 8, 128), 0) * 8
                    rows = rows + lax.broadcasted_iota(jnp.int32, (CHUNK, 8, 128), 1)
                    cols = lax.broadcasted_iota(jnp.int32, (CHUNK, 8, 128), 2) + half * 128
                    dist_sq = jnp.where(rows == cols, 1.0, dist_sq)
                inverse = lax.rsqrt(dist_sq)
                inside = jnp.maximum(1.0 - dist_sq, 0.0)
                inverse_sq = inverse * inverse
                radial = (inside * inside) * inverse * inverse_sq
                cubed = dist_sq * dist_sq * inverse
                power = (target[4, at] + source[5]) * (target[3, at] * source[4]) * cubed
                decay = jnp.exp2(power)
                three = 1.0 - decay
                five = three + (power * LN2) * decay
                direct = radial * three
                coef_b[k, at, :, lanes] = direct
                coef_a[k, at, :, lanes] = (radial * 3.0) * inverse_sq * five
                weight = jnp.where(target[5, at] != source[6], direct * source[3], 0.0)
                for d in range(3):
                    if own and half == 0:
                        totals[d, at] = weight * deltas[d]
                    else:
                        totals[d, at] += weight * deltas[d]
                return carry

            lax.fori_loop(0, GROUPS // CHUNK, chunk, 0, unroll=True)

    geometry(0, True)

    def static_box(k, carry):
        static_copy(k, k, mine).wait_recv()
        for d, step in enumerate((lax.rem(k, 3), lax.rem(k // 3, 3), k // 9)):
            moved = code_offset(step).astype(jnp.float32) * SCALE
            places[k, d : d + 1] = statics[k, d : d + 1] + moved
        geometry(k, False)
        return carry

    lax.fori_loop(1, 27, static_box, 0)

    permanent = [lane_sums(totals[d]) for d in range(3)]
    permanent = jnp.concatenate(permanent, axis=0)
    to_shift = jnp.where(live, DRUDE_GAIN * drude, 0.0)
    to_moment = to_shift * drude * (1.0 / CUTOFF**3)

    def induced(turn, k):
        mu = [moments[turn, k, d : d + 1] for d in range(3)]
        xs = [places[k, d : d + 1] for d in range(3)]
        along = xs[0] * mu[0] + xs[1] * mu[1] + xs[2] * mu[2]
        for half in range(2):
            lanes = pl.ds(half * 128, 128)
            sl = slice(half * 128, half * 128 + 128)
            m = [spread(moments[turn, k, d : d + 1, lanes]) for d in range(3)]
            x = [spread(places[k, d : d + 1, lanes]) for d in range(3)]
            s = spread(along[:, sl])

            def chunk(c, carry, lanes=lanes, m=m, x=x, s=s):
                at = pl.ds(c * CHUNK, CHUNK)
                proj = target[0, at] * m[0] + target[1, at] * m[1] + target[2, at] * m[2] - s
                dipolar = coef_a[k, at, :, lanes] * proj
                direct = coef_b[k, at, :, lanes]
                totals[3, at] += dipolar
                for d in range(3):
                    totals[d, at] += dipolar * x[d] + direct * m[d]
                return carry

            lax.fori_loop(0, GROUPS // CHUNK, chunk, 0, unroll=True)

    def turn_body(turn, fields):
        moments[turn, 0] = jnp.concatenate([to_moment * fields, jnp.zeros((1, SLOTS), jnp.float32)], axis=0)
        for k in range(26, 0, -1):
            moment_copy(turn, k, mirror[k], peers[k]).start()
        totals[...] = jnp.zeros_like(totals)

        def moment_box(k, carry):
            @pl.when(k > 0)
            def _():
                moment_copy(turn, k, k, mine).wait_recv()

            induced(turn, k)
            return carry

        lax.fori_loop(0, 27, moment_box, 0)
        plain = lane_sums(totals[3])
        rows = [place[d : d + 1] * plain - lane_sums(totals[d]) for d in range(3)]
        return permanent + jnp.concatenate(rows, axis=0)

    before = lax.fori_loop(0, ITERS - 1, turn_body, permanent)
    fields = turn_body(ITERS - 1, before)
    shifts = to_shift * before

    def drain(k, carry):
        static_copy(k, k, mine).wait_send()
        for turn in range(ITERS):
            moment_copy(turn, k, k, mine).wait_send()
        return carry

    velocity = velocity_ref[0, 0, 0] + KICK * charge * fields / masses_ref[0, 0]
    moved = fractions + (TIMESTEP / EDGE) * velocity

    lists = leaving_ref[0, 0, 0].astype(jnp.float32)
    lane = lax.broadcasted_iota(jnp.int32, (MOVE, 128), 1)
    pick = jnp.where(lax.rem(lane, MOVE) == lax.broadcasted_iota(jnp.int32, (MOVE, 128), 0), 1.0, 0.0)
    tiled = jnp.dot(lists, pick, precision=HIGHEST, preferred_element_type=jnp.float32)
    lane6 = lax.broadcasted_iota(jnp.int32, (6, 128), 1)
    mine6 = lane6 // MOVE == lax.broadcasted_iota(jnp.int32, (6, 128), 0)
    flat = jnp.sum(jnp.where(mine6, tiled, 0.0), axis=0, keepdims=True)
    lane1 = lax.broadcasted_iota(jnp.int32, (1, 128), 1)
    flat = jnp.where(lane1 < 6 * MOVE, flat, -1.0)
    slot_rows = lax.broadcasted_iota(jnp.int32, (SLOTS, 128), 0).astype(jnp.float32)
    matches = jnp.where(slot_rows == flat, 1.0, 0.0)
    named = lax.dot_general(
        jnp.ones((8, 128), jnp.float32),
        matches,
        (((1,), (1,)), ((), ())),
        preferred_element_type=jnp.float32,
    )[0:1]
    present = jnp.where(flat >= 0.0, 1.0, 0.0)

    complete = jnp.concatenate(
        [
            moved,
            velocity,
            shifts,
            charge,
            drude,
            screening,
            label,
            masses_ref[0, 0],
            jnp.zeros((2, SLOTS), jnp.float32),
        ],
        axis=0,
    )
    packed = jnp.dot(complete, matches, precision=HIGHEST, preferred_element_type=jnp.float32)
    face = lane1 // MOVE
    headings = []
    for d in range(3):
        heading = jnp.where(face == 2 * d, -1.0, 0.0) + jnp.where(face == 2 * d + 1, 1.0, 0.0)
        headings.append(heading * present)
    headings.append(jnp.zeros((13, 128), jnp.float32))
    outbox[...] = packed + jnp.concatenate(headings, axis=0)

    def out_copy(face, device):
        return pltpu.make_async_remote_copy(
            src_ref=outbox,
            dst_ref=inbox.at[face],
            send_sem=out_send.at[face],
            recv_sem=out_recv.at[face],
            device_id=device,
            device_id_type=MESH,
        )

    for at in range(5, -1, -1):
        out_copy(at, step_from(mine, sizes, UNITS[at])).start()
    remain = jnp.logical_and(live, named < 0.5)
    staying_ref[0, 0, 0] = jnp.where(remain, complete[0:9], 0.0)
    lax.fori_loop(1, 27, drain, 0)
    landed = jnp.zeros((16, 128), jnp.float32)
    lane16 = lax.broadcasted_iota(jnp.int32, (16, 128), 1) // MOVE
    for at in range(6):
        out_copy(at, mine).wait_recv()
        landed = jnp.where(lane16 == at, inbox[at], landed)
    arrivals_ref[0, 0, 0] = landed[0:14, 0 : 6 * MOVE]
    for at in range(6):
        out_copy(at, mine).wait_send()


def solution(mesh):
    sizes = tuple(mesh.shape[axis] for axis in AXES)
    vec = P("gx", "gy", "gz", None, None)
    row = P("gx", "gy", "gz", None)
    placed = (vec, vec, row, row, row, row, row, P("gx", "gy", "gz"), vec)
    vmem = pl.BlockSpec(memory_space=pltpu.VMEM)
    smem = pl.BlockSpec(memory_space=pltpu.SMEM)
    call = pl.pallas_call(
        functools.partial(kernel, sizes),
        out_shape=(
            jax.ShapeDtypeStruct((1, 1, 1, 9, SLOTS), jnp.float32),
            jax.ShapeDtypeStruct((1, 1, 1, 14, 6 * MOVE), jnp.float32),
        ),
        in_specs=[smem] + [vmem] * 8,
        out_specs=(vmem, vmem),
        scratch_shapes=[
            pltpu.VMEM((27, 8, SLOTS), jnp.float32),
            pltpu.VMEM((27, 4, SLOTS), jnp.float32),
            pltpu.VMEM((ITERS, 27, 4, SLOTS), jnp.float32),
            pltpu.VMEM((6, GROUPS, 8, 128), jnp.float32),
            pltpu.VMEM((27, GROUPS, 8, SLOTS), jnp.float32),
            pltpu.VMEM((27, GROUPS, 8, SLOTS), jnp.float32),
            pltpu.VMEM((4, GROUPS, 8, 128), jnp.float32),
            pltpu.VMEM((16, 128), jnp.float32),
            pltpu.VMEM((6, 16, 128), jnp.float32),
            pltpu.SemaphoreType.DMA((27,)),
            pltpu.SemaphoreType.DMA((27,)),
            pltpu.SemaphoreType.DMA((ITERS, 27)),
            pltpu.SemaphoreType.DMA((ITERS, 27)),
            pltpu.SemaphoreType.DMA((6,)),
            pltpu.SemaphoreType.DMA((6,)),
        ],
        compiler_params=pltpu.CompilerParams(
            collective_id=0, has_side_effects=True, vmem_limit_bytes=40 * 1024 * 1024
        ),
    )

    def local(fractions, velocity, charge, drude_charge, screening, labels, masses, counts, leaving):
        return call(
            counts, fractions, velocity, charge, drude_charge, screening, labels, masses, leaving
        )

    return jax.shard_map(local, mesh=mesh, in_specs=placed, out_specs=(vec, vec), check_vma=False)
```

profile of v0, /device:TPU:1, one launch (start us, length us, event | category | flops | bytes accessed | tf_op | source)
XLA Modules:
  0.0 61.3 jit_solution(2929708748223496529)
XLA Ops:
  1.3 0.0 copy-start.5
  1.3 0.7 %copy.11.fractions_ref = f32[1,1,1,3,256]{4,3,2,1,0:T(4,128)S(1)} copy(f32[1,1,1,3,256]{4,2,3,1,0:T(1,128)} %param.9) | data formatting | bytes 6144 | tf_op args[0]
  2.0 0.0 copy-done.5
  2.0 0.0 copy-start.6
  2.0 0.7 %copy-done.6 = s32[1,1,1,6,16]{4,2,3,1,0:T(1,128)S(1)} copy-done((s32[1,1,1,6,16]{4,2,3,1,0:T(1,128)S(1)}, s32[1,1,1,6,16]{4,2,3,1,0:T(1,128)}, u32[]{:S(2)}) %copy-start.6) | copy-done | bytes 408
  2.7 0.0 copy-start
  2.7 0.0 copy-start.1
  2.7 0.0 copy-start.2
  2.7 0.0 copy-start.3
  2.7 0.0 copy-start.4
  2.7 0.6 %copy-done = f32[1,1,1,256]{3,2,1,0:T(1,128)S(1)} copy-done((f32[1,1,1,256]{3,2,1,0:T(1,128)S(1)}, f32[1,1,1,256]{3,2,1,0:T(1,128)}, u32[]{:S(2)}) %copy-start) | copy-done | bytes 1048
  3.3 0.0 copy-done.1
  3.4 0.0 copy-done.2
  3.4 0.0 copy-done.3
  3.4 0.0 copy-done.4
  3.4 56.7 %shard_map.104 = (f32[1,1,1,9,256]{4,3,2,1,0:T(8,128)S(1)}, f32[1,1,1,14,96]{4,3,2,1,0:T(8,128)S(1)}) custom-call(s32[1,1,1]{2,1,0:T(1,128)S(6)} %copy.16.counts_ref, f32[1,1,1,3,256]{4,3,2,1,0:T(4,128)S(1)} %copy.11.fractions_ref, f32[1,1,1,3,256]{4,3,2,1,0:T(4,128)S(1)} %copy.12.velocity_ref, f32[1,1,1,256]{3,2,1,0:T(1,128)S(1)} %copy-done, ...), custom_call_target="tpu_custom_call" | custom-call | tf_op jit(solution)/shard_map/pallas_call | solution.py:345
  60.1 0.6 copy.14
  60.7 0.6 copy.15
  (2 shorter events, 0.0 us)
Async XLA Ops:
  1.3 0.7 %copy-start.5 = (f32[1,1,1,3,256]{4,2,3,1,0:T(1,128)S(1)}, f32[1,1,1,3,256]{4,2,3,1,0:T(1,128)}, u32[]{:S(2)}) copy-start(f32[1,1,1,3,256]{4,2,3,1,0:T(1,128)} %param.10) | copy-start | bytes 9220
  2.0 0.7 %copy-start.6 = (s32[1,1,1,6,16]{4,2,3,1,0:T(1,128)S(1)}, s32[1,1,1,6,16]{4,2,3,1,0:T(1,128)}, u32[]{:S(2)}) copy-start(s32[1,1,1,6,16]{4,2,3,1,0:T(1,128)} %param.17) | copy-start | bytes 1156
  2.7 0.7 %copy-start = (f32[1,1,1,256]{3,2,1,0:T(1,128)S(1)}, f32[1,1,1,256]{3,2,1,0:T(1,128)}, u32[]{:S(2)}) copy-start(f32[1,1,1,256]{3,2,1,0:T(1,128)} %charge_ref.1) | copy-start | bytes 3076
  2.7 0.7 %copy-start.1 = (f32[1,1,1,256]{3,2,1,0:T(1,128)S(1)}, f32[1,1,1,256]{3,2,1,0:T(1,128)}, u32[]{:S(2)}) copy-start(f32[1,1,1,256]{3,2,1,0:T(1,128)} %drude_ref.1) | copy-start | bytes 3076
  2.7 0.7 %copy-start.2 = (f32[1,1,1,256]{3,2,1,0:T(1,128)S(1)}, f32[1,1,1,256]{3,2,1,0:T(1,128)}, u32[]{:S(2)}) copy-start(f32[1,1,1,256]{3,2,1,0:T(1,128)} %screening_ref.1) | copy-start | bytes 3076
  2.7 0.7 %copy-start.3 = (s32[1,1,1,256]{3,2,1,0:T(1,128)S(1)}, s32[1,1,1,256]{3,2,1,0:T(1,128)}, u32[]{:S(2)}) copy-start(s32[1,1,1,256]{3,2,1,0:T(1,128)} %labels_ref.1) | copy-start | bytes 3076
  2.7 0.7 %copy-start.4 = (f32[1,1,1,256]{3,2,1,0:T(1,128)S(1)}, f32[1,1,1,256]{3,2,1,0:T(1,128)}, u32[]{:S(2)}) copy-start(f32[1,1,1,256]{3,2,1,0:T(1,128)} %masses_ref.1) | copy-start | bytes 3076
where the time goes:
time: 61.5 us; the launch traced here: 61.3 us
  Pallas kernels  56.7 us (92%)
  local copies, waits for them, and re-layouts  3.31 us (5%)
  between operations  1.32 us (2%)
    pallas_call x1, Pallas kernels, local(): call(counts, fractions, velocity, charge, drude_charge, screening, labels...  56.7 us
    unnamed x17, local copies, waits for them, and re-layouts  2.1 us

commit v1 on v0

v1 whole, which is shorter than its diff:
```python
import functools
import math

import jax
import jax.numpy as jnp
from jax import lax
from jax.experimental import pallas as pl
from jax.experimental.pallas import tpu as pltpu
from jax.sharding import PartitionSpec as P

SLOTS = 256
MOVE = 16
ITERS = 3
CUTOFF = 12.0
DRUDE_GAIN = 0.3320636
KICK = 0.002 * 418.4 * 332.0636
TIMESTEP = 0.002
UNITS = ((1, 0, 0), (-1, 0, 0), (0, 1, 0), (0, -1, 0), (0, 0, 1), (0, 0, -1))
EDGE = max(12.0, (10.0 * SLOTS) ** (1.0 / 3.0))
SCALE = EDGE / CUTOFF
LN2 = math.log(2.0)
GROUPS = SLOTS // 8
CHUNK = 4
AXES = ("gx", "gy", "gz")
MESH = pl.DeviceIdType.MESH
HIGHEST = lax.Precision.HIGHEST
F32 = jnp.float32
BF16 = jnp.bfloat16


def code_offset(code):
    return (code + 1) % 3 - 1 if isinstance(code, int) else lax.rem(code + 1, 3) - 1


def step_from(mine, sizes, step):
    return tuple(lax.rem(mine[a] + (step[a] + sizes[a]), sizes[a]) for a in range(3))


def columns(row):
    return jnp.transpose(jnp.broadcast_to(row, (128, SLOTS))).reshape(GROUPS, 8, 128)


def split(value):
    high = value.astype(BF16)
    return high, value - high.astype(F32)


def kernel(
    sizes,
    fractions_hbm,
    velocity_hbm,
    charge_hbm,
    drude_hbm,
    screening_hbm,
    labels_hbm,
    masses_hbm,
    counts_hbm,
    leaving_hbm,
    staying_ref,
    arrivals_ref,
    fractions_ref,
    velocity_ref,
    charge_ref,
    drude_ref,
    screening_ref,
    labels_ref,
    masses_ref,
    counts_ref,
    leaving_ref,
    statics,
    places,
    moments,
    even,
    odd,
    coef_a,
    coef_b,
    totals,
    sums_a,
    sums_b,
    chosen,
    latest,
    outbox,
    inbox,
    load_sem,
    static_send,
    static_recv,
    moment_send,
    moment_recv,
    out_send,
    out_recv,
):
    mine = tuple(lax.axis_index(axis) for axis in AXES)
    steps = [(code_offset(k % 3), code_offset(k // 3 % 3), code_offset(k // 9)) for k in range(27)]
    peers = [step_from(mine, sizes, step) for step in steps]
    mirror = [(3 - k % 3) % 3 + 3 * ((3 - k // 3 % 3) % 3) + 9 * ((3 - k // 9) % 3) for k in range(27)]

    barrier = pltpu.get_barrier_semaphore()
    for k in range(26, 0, -1):
        pl.semaphore_signal(barrier, inc=1, device_id=peers[k], device_id_type=MESH)

    pairs = (
        (fractions_hbm, fractions_ref),
        (charge_hbm, charge_ref),
        (drude_hbm, drude_ref),
        (screening_hbm, screening_ref),
        (labels_hbm, labels_ref),
        (counts_hbm, counts_ref),
        (velocity_hbm, velocity_ref),
        (masses_hbm, masses_ref),
        (leaving_hbm, leaving_ref),
    )
    loads = [pltpu.make_async_copy(src, dst, load_sem.at[at]) for at, (src, dst) in enumerate(pairs)]
    for load in loads:
        load.start()
    for load in loads:
        load.wait()

    slots = lax.broadcasted_iota(jnp.int32, (1, SLOTS), 1)
    live = slots < jnp.broadcast_to(counts_ref[0], (1, SLOTS))
    fractions = [fractions_ref[d] for d in range(3)]
    charge = jnp.where(live, charge_ref[0], 0.0)
    drude = jnp.where(live, drude_ref[0], -1.0)
    screening = screening_ref[0]
    label = labels_ref[0].astype(F32)
    place = [(fractions[d] - 0.5) * SCALE for d in range(3)]
    root = math.sqrt(0.5 * CUTOFF**3 / LN2) * lax.rsqrt(DRUDE_GAIN * drude * drude)
    own_rows = place + [root, screening, label, charge * (1.0 / CUTOFF**2)]
    for at, row in enumerate(own_rows):
        statics[0, at : at + 1] = row
    statics[0, 7:8] = jnp.zeros((1, SLOTS), F32)
    for d in range(3):
        places[0, d : d + 1] = place[d]

    pl.semaphore_wait(barrier, 26)

    def static_copy(slot, device):
        return pltpu.make_async_remote_copy(
            src_ref=statics.at[0],
            dst_ref=statics.at[slot],
            send_sem=static_send,
            recv_sem=static_recv.at[(slot - 1) // 2],
            device_id=device,
            device_id_type=MESH,
        )

    def moment_group(slot):
        return 0 if slot < 5 else slot // 9 + (1 if slot < 9 else 1)

    def moment_copy(turn, slot, device):
        return pltpu.make_async_remote_copy(
            src_ref=moments.at[turn, 0],
            dst_ref=moments.at[turn, slot],
            send_sem=moment_send.at[turn],
            recv_sem=moment_recv.at[turn, moment_group(slot)],
            device_id=device,
            device_id_type=MESH,
        )

    def landed(ref, sem):
        pltpu.make_async_copy(ref, ref, sem).wait()

    for k in range(26, 0, -1):
        static_copy(mirror[k], peers[k]).start()

    def fill(k, buffer):
        for at in range(6):
            buffer[at] = columns(places[k, at : at + 1] if at < 3 else statics[k, at : at + 1])
        buffer[6] = columns(statics[k, 6:7])

    def spread(row, half):
        return jnp.broadcast_to(row[:, half * 128 : half * 128 + 128], (8, 128))

    def geometry(k, buffer, own):
        sums = [None] * 6
        for half in range(2):
            goal = [spread(row, half) for row in place + [-root, screening, label]]
            for c in range(GROUPS // CHUNK):
                at = pl.ds(c * CHUNK, CHUNK)
                deltas = [goal[d] - buffer[d, at] for d in range(3)]
                dist_sq = deltas[0] * deltas[0] + deltas[1] * deltas[1] + deltas[2] * deltas[2]
                if own:
                    rows = c * (CHUNK * 8) + lax.broadcasted_iota(jnp.int32, (CHUNK, 8, 128), 0) * 8
                    rows = rows + lax.broadcasted_iota(jnp.int32, (CHUNK, 8, 128), 1)
                    cols = lax.broadcasted_iota(jnp.int32, (CHUNK, 8, 128), 2) + half * 128
                    dist_sq = jnp.where(rows == cols, 1.0, dist_sq)
                inverse = lax.rsqrt(dist_sq)
                inside = jnp.maximum(1.0 - dist_sq, 0.0)
                inverse_sq = inverse * inverse
                radial = (inside * inside) * inverse * inverse_sq
                cubed = dist_sq * dist_sq * inverse
                power = (goal[4] + buffer[4, at]) * (goal[3] * buffer[3, at]) * cubed
                decay = jnp.exp2(power)
                three = 1.0 - decay
                five = three + (power * LN2) * decay
                direct = radial * three
                coef_b[k, at, :, pl.ds(half * 128, 128)] = direct
                coef_a[k, at, :, pl.ds(half * 128, 128)] = radial * inverse_sq * five
                weight = jnp.where(goal[5] != buffer[5, at], direct * buffer[6, at], 0.0)
                for d in range(3):
                    term = jnp.sum(weight * deltas[d], axis=0)
                    old = sums[3 * half + d]
                    sums[3 * half + d] = term if old is None else old + term
        for half in range(2):
            for d in range(3):
                lanes = pl.ds(half * 128, 128)
                if own:
                    totals[d, :, lanes] = sums[3 * half + d]
                else:
                    totals[d, :, lanes] += sums[3 * half + d]

    def arrive(k):
        for d, step in enumerate((lax.rem(k, 3), lax.rem(k // 3, 3), k // 9)):
            moved = code_offset(step).astype(F32) * SCALE
            places[k, d : d + 1] = statics[k, d : d + 1] + moved

    fill(0, even)
    geometry(0, even, True)

    def wait_pair(p):
        landed(statics.at[pl.ds(2 * p + 1, 2)], static_recv.at[p])
        arrive(2 * p + 1)
        arrive(2 * p + 2)

    wait_pair(jnp.int32(0))
    fill(1, odd)

    def box_pair(p, carry):
        k = 2 * p + 1
        fill(k + 1, even)
        geometry(k, odd, False)

        @pl.when(p < 12)
        def _():
            wait_pair(p + 1)

        fill(jnp.minimum(k + 2, 26), odd)
        geometry(k + 1, even, False)
        return carry

    lax.fori_loop(0, 13, box_pair, 0)

    permanent = [jnp.sum(totals[d], axis=0, keepdims=True) for d in range(3)]
    to_shift = jnp.where(live, DRUDE_GAIN * drude, 0.0)
    to_moment = to_shift * drude * (1.0 / CUTOFF**3)

    def induced(turn, boxes, first):
        part_a = part_b = None
        for k in boxes:
            mu = [moments[turn, k, d : d + 1] for d in range(3)]
            at = [places[k, d : d + 1] for d in range(3)]
            along = at[0] * mu[0] + at[1] * mu[1] + at[2] * mu[2]
            rows = mu + [along]
            rows += [mu[d] * at[e] for e in range(3) for d in range(3)]
            rows += [along * at[e] for e in range(3)]
            high, rest = split(jnp.concatenate(rows, axis=0))
            middle, rest = split(rest)
            left = jnp.concatenate([high, middle, rest.astype(BF16)], axis=0)

            def through(coef, part, k=k, left=left):
                high, low = split(coef[k].reshape(SLOTS, SLOTS))
                for right in (high, low.astype(BF16)):
                    term = jnp.dot(left, right, preferred_element_type=F32)
                    part = term if part is None else part + term
                return part

            part_a = through(coef_a, part_a)
            part_b = through(coef_b, part_b)
        if first:
            sums_a[...] = part_a
            sums_b[...] = part_b
        else:
            sums_a[...] += part_a
            sums_b[...] += part_b

    near = jnp.where(lax.rem(mine[2], 4) == 3, 2, 1)

    def choose():
        lane1 = lax.broadcasted_iota(jnp.int32, (1, 128), 1)
        lane = lax.broadcasted_iota(jnp.int32, (MOVE, 128), 1)
        pick = lax.rem(lane, MOVE) == lax.broadcasted_iota(jnp.int32, (MOVE, 128), 0)
        pick = jnp.where(pick, 1.0, 0.0)
        flat = jnp.full((1, 128), -1.0, F32)
        for at in range(6):
            tiled = jnp.dot(
                jnp.broadcast_to(leaving_ref[at].astype(F32), (8, MOVE)),
                pick,
                precision=HIGHEST,
                preferred_element_type=F32,
            )[0:1]
            flat = jnp.where(lane1 // MOVE == at, tiled, flat)
        slot_rows = lax.broadcasted_iota(jnp.int32, (SLOTS, 128), 0).astype(F32)
        chosen[0:SLOTS] = jnp.where(slot_rows == flat, 1.0, 0.0)
        chosen[SLOTS : SLOTS + 8] = jnp.broadcast_to(flat, (8, 128))

    for d in range(3):
        latest[3 + d : 4 + d] = permanent[d]
        latest[6 + d : 7 + d] = permanent[d]

    def turn_body(turn, carry):
        for d in range(3):
            field = latest[3 + d : 4 + d]
            latest[d : d + 1] = field
            moments[turn, 0, d : d + 1] = to_moment * field
        moments[turn, 0, 3:4] = jnp.zeros((1, SLOTS), F32)
        for k in range(26, 0, -1):
            moment_copy(turn, mirror[k], peers[k]).start()
        induced(turn, [0], True)

        @pl.when(turn == 0)
        def _():
            choose()

        landed(moments.at[turn, pl.ds(1, 4)], moment_recv.at[turn, 0])
        induced(turn, [1, 2, 3, 4], False)
        landed(moments.at[turn, pl.ds(5, 4)], moment_recv.at[turn, 1])
        induced(turn, [5, 6, 7, 8], False)
        for side in (near, 3 - near):
            landed(moments.at[turn, pl.ds(side * 9, 9)], moment_recv.at[turn, side + 1])
            induced(turn, [side * 9 + at for at in range(9)], False)
        landed(moments.at[turn, pl.ds(1, 26)], moment_send.at[turn])
        tall, wide = sums_a[...], sums_b[...]
        tall = tall[0:16] + tall[16:32] + tall[32:48]
        wide = wide[0:16] + wide[16:32] + wide[32:48]
        plain = place[0] * tall[0:1] + place[1] * tall[1:2] + place[2] * tall[2:3] - tall[3:4]
        for e in range(3):
            mixed = [place[d] * tall[4 + 3 * e + d : 5 + 3 * e + d] for d in range(3)]
            dipolar = place[e] * plain - (mixed[0] + mixed[1] + mixed[2]) + tall[13 + e : 14 + e]
            latest[3 + e : 4 + e] = latest[6 + e : 7 + e] + 3.0 * dipolar - wide[e : e + 1]
        return carry

    lax.fori_loop(0, ITERS, turn_body, 0)
    before = [latest[d : d + 1] for d in range(3)]
    fields = [latest[3 + d : 4 + d] for d in range(3)]
    shifts = [to_shift * before[d] for d in range(3)]

    mass = masses_ref[0]
    velocity = [velocity_ref[d] + KICK * charge * fields[d] / mass for d in range(3)]
    moved = [fractions[d] + (TIMESTEP / EDGE) * velocity[d] for d in range(3)]
    rows = moved + velocity + shifts
    rest = [charge, drude, screening, label, mass, jnp.zeros((2, SLOTS), F32)]
    complete = jnp.concatenate(rows + rest, axis=0)
    matches = chosen[0:SLOTS]
    flat = chosen[SLOTS : SLOTS + 1]
    packed = jnp.dot(complete, matches, precision=HIGHEST, preferred_element_type=F32)
    present = jnp.where(flat >= 0.0, 1.0, 0.0)
    face = lax.broadcasted_iota(jnp.int32, (1, 128), 1) // MOVE
    headings = []
    for d in range(3):
        heading = jnp.where(face == 2 * d, -1.0, 0.0) + jnp.where(face == 2 * d + 1, 1.0, 0.0)
        headings.append(heading * present)
    headings.append(jnp.zeros((13, 128), F32))
    outbox[...] = packed + jnp.concatenate(headings, axis=0)

    def out_copy(face, device):
        return pltpu.make_async_remote_copy(
            src_ref=outbox,
            dst_ref=inbox.at[face],
            send_sem=out_send,
            recv_sem=out_recv,
            device_id=device,
            device_id_type=MESH,
        )

    for at in range(5, -1, -1):
        out_copy(at, step_from(mine, sizes, UNITS[at])).start()
    named = lax.dot_general(
        jnp.ones((8, 128), F32), matches, (((1,), (1,)), ((), ())), preferred_element_type=F32
    )[0:1]
    remain = jnp.logical_and(live, named < 0.5)
    for at in range(9):
        staying_ref[at] = jnp.where(remain, rows[at], 0.0)
    landed(statics.at[pl.ds(1, 26)], static_send)
    landed(inbox, out_recv)
    result = jnp.zeros((16, 128), F32)
    lane16 = lax.broadcasted_iota(jnp.int32, (16, 128), 1) // MOVE
    for at in range(6):
        result = jnp.where(lane16 == at, inbox[at], result)
    for at in range(14):
        arrivals_ref[at] = result[at : at + 1, 0 : 6 * MOVE]
    landed(inbox, out_send)


def solution(mesh):
    sizes = tuple(mesh.shape[axis] for axis in AXES)
    vec = P("gx", "gy", "gz", None, None)
    row = P("gx", "gy", "gz", None)
    placed = (vec, vec, row, row, row, row, row, P("gx", "gy", "gz"), vec)
    vmem = pl.BlockSpec(memory_space=pltpu.VMEM)
    hbm = pl.BlockSpec(memory_space=pltpu.HBM)
    call = pl.pallas_call(
        functools.partial(kernel, sizes),
        out_shape=(
            jax.ShapeDtypeStruct((9, 1, SLOTS), F32),
            jax.ShapeDtypeStruct((14, 1, 6 * MOVE), F32),
        ),
        in_specs=[hbm] * 9,
        out_specs=(vmem, vmem),
        scratch_shapes=[
            pltpu.VMEM((3, 1, SLOTS), F32),
            pltpu.VMEM((3, 1, SLOTS), F32),
            pltpu.VMEM((1, 1, SLOTS), F32),
            pltpu.VMEM((1, 1, SLOTS), F32),
            pltpu.VMEM((1, 1, SLOTS), F32),
            pltpu.VMEM((1, 1, SLOTS), jnp.int32),
            pltpu.VMEM((1, 1, SLOTS), F32),
            pltpu.VMEM((1, 1, 1), jnp.int32),
            pltpu.VMEM((6, 1, MOVE), jnp.int32),
            pltpu.VMEM((27, 8, SLOTS), F32),
            pltpu.VMEM((27, 4, SLOTS), F32),
            pltpu.VMEM((ITERS, 27, 4, SLOTS), F32),
            pltpu.VMEM((7, GROUPS, 8, 128), F32),
            pltpu.VMEM((7, GROUPS, 8, 128), F32),
            pltpu.VMEM((27, GROUPS, 8, SLOTS), F32),
            pltpu.VMEM((27, GROUPS, 8, SLOTS), F32),
            pltpu.VMEM((3, 8, SLOTS), F32),
            pltpu.VMEM((48, SLOTS), F32),
            pltpu.VMEM((48, SLOTS), F32),
            pltpu.VMEM((SLOTS + 8, 128), F32),
            pltpu.VMEM((16, SLOTS), F32),
            pltpu.VMEM((16, 128), F32),
            pltpu.VMEM((6, 16, 128), F32),
            pltpu.SemaphoreType.DMA((9,)),
            pltpu.SemaphoreType.DMA,
            pltpu.SemaphoreType.DMA((13,)),
            pltpu.SemaphoreType.DMA((ITERS,)),
            pltpu.SemaphoreType.DMA((ITERS, 4)),
            pltpu.SemaphoreType.DMA,
            pltpu.SemaphoreType.DMA,
        ],
        compiler_params=pltpu.CompilerParams(
            collective_id=0, has_side_effects=True, vmem_limit_bytes=67043328
        ),
    )

    def local(fractions, velocity, charge, drude_charge, screening, labels, masses, counts, leaving):
        flat = [value.reshape(1, 1, SLOTS) for value in (charge, drude_charge, screening, labels, masses)]
        staying, arrivals = call(
            fractions.reshape(3, 1, SLOTS),
            velocity.reshape(3, 1, SLOTS),
            *flat,
            counts,
            leaving.reshape(6, 1, MOVE),
        )
        return staying.reshape(1, 1, 1, 9, SLOTS), arrivals.reshape(1, 1, 1, 14, 6 * MOVE)

    return jax.shard_map(local, mesh=mesh, in_specs=placed, out_specs=(vec, vec), check_vma=False)
```

time: 61.5 us -> 56.2 us (0.914)
  Pallas kernels: 56.7 us -> 52.8 us
  local copies, waits for them, and re-layouts: 3.31 us -> 1.9 us
    pallas_call x1, Pallas kernels: 56.7 us -> 52.8 us  [local(): call(fractions.reshape(3, 1, SLOTS), velocity.reshape(3, 1, SLOTS), *flat...]
    pallas_call x2 -> x0, local copies, waits for them, and re-layouts: 1.21 us -> none  [local(): call(counts, fractions, velocity, charge, drude_charge, screening, labels...]
    unnamed x17 -> x4, local copies, waits for them, and re-layouts: 2.1 us -> 1.9 us
where the time goes in v1:
time: 56.2 us; the launch traced here: 56 us
  Pallas kernels  52.8 us (94%)
  local copies, waits for them, and re-layouts  1.9 us (3%)
  between operations  1.3 us (2%)
    pallas_call x1, Pallas kernels, local(): call(fractions.reshape(3, 1, SLOTS), velocity.reshape(3, 1, SLOTS), *flat...  52.8 us
    unnamed x4, local copies, waits for them, and re-layouts  1.9 us

profile of v1, /device:TPU:1, one launch (start us, length us, event | category | flops | bytes accessed | tf_op | source)
XLA Modules:
  0.0 56.0 jit_solution(18276601444004981308)
XLA Ops:
  1.3 52.8 %shard_map.104 = (f32[9,1,256]{2,1,0:T(1,128)}, f32[14,1,96]{2,1,0:T(1,128)}) custom-call(f32[3,1,256]{2,1,0:T(1,128)} %bitcast.16, f32[3,1,256]{2,1,0:T(1,128)} %bitcast.17, f32[1,1,256]{2,1,0:T(1,128)} %bitcast.19, f32[1,1,256]{2,1,0:T(1,128)} %bitcast.20, f32[1,1,256]{2,1,0:T(1,128)} %bitcast.21, s32[1,1,256]{2,1,0:T(1,128)} %bitcast.22, ...), custom_call_target="tpu_custom_call" | custom-call | tf_op jit(solution)/shard_map/pallas_call | solution.py:437
  54.1 0.0 copy-start
  54.1 1.3 %copy.16 = f32[1,1,1,9,256]{4,2,3,1,0:T(1,128)} copy(f32[1,1,1,9,256]{4,2,3,1,0:T(1,128)} %bitcast.14) | data formatting | bytes 18432
  55.4 0.0 copy-done
  55.4 0.6 %copy.17 = f32[1,1,1,14,96]{4,2,3,1,0:T(1,128)} copy(f32[1,1,1,14,96]{4,2,3,1,0:T(1,128)S(1)} %bitcast.15) | data formatting | bytes 10752
Async XLA Ops:
  54.1 1.3 %copy-start = (f32[14,1,96]{2,1,0:T(1,128)S(1)}, f32[14,1,96]{2,1,0:T(1,128)}, u32[]{:S(2)}) copy-start(f32[14,1,96]{2,1,0:T(1,128)} %get-tuple-element.5) | copy-start | bytes 16132

commit v2 on v1

--- a/solution.py
+++ b/solution.py
@@ -20,6 +20,7 @@
 SCALE = EDGE / CUTOFF
 LN2 = math.log(2.0)
 GROUPS = SLOTS // 8
+LAYER = ((0, 0), (1, 0), (-1, 0), (0, 1), (0, -1), (1, 1), (-1, -1), (1, -1), (-1, 1))
 CHUNK = 4
 AXES = ("gx", "gy", "gz")
 MESH = pl.DeviceIdType.MESH
@@ -72,9 +73,12 @@
     moments,
     even,
     odd,
+    even_damping,
+    odd_damping,
+    even_weights,
+    odd_weights,
     coef_a,
     coef_b,
-    totals,
     sums_a,
     sums_b,
     chosen,
@@ -90,9 +94,9 @@
     out_recv,
 ):
     mine = tuple(lax.axis_index(axis) for axis in AXES)
-    steps = [(code_offset(k % 3), code_offset(k // 3 % 3), code_offset(k // 9)) for k in range(27)]
+    steps = [(x, y, code_offset(k // 9)) for k, (x, y) in enumerate(LAYER * 3)]
     peers = [step_from(mine, sizes, step) for step in steps]
-    mirror = [(3 - k % 3) % 3 + 3 * ((3 - k // 3 % 3) % 3) + 9 * ((3 - k // 9) % 3) for k in range(27)]
+    mirror = [steps.index((-x, -y, -z)) for x, y, z in steps]
 
     barrier = pltpu.get_barrier_semaphore()
     for k in range(26, 0, -1):
@@ -124,7 +128,7 @@
     label = labels_ref[0].astype(F32)
     place = [(fractions[d] - 0.5) * SCALE for d in range(3)]
     root = math.sqrt(0.5 * CUTOFF**3 / LN2) * lax.rsqrt(DRUDE_GAIN * drude * drude)
-    own_rows = place + [root, screening, label, charge * (1.0 / CUTOFF**2)]
+    own_rows = place + [label, root, screening * root, charge * (1.0 / CUTOFF**2)]
     for at, row in enumerate(own_rows):
         statics[0, at : at + 1] = row
     statics[0, 7:8] = jnp.zeros((1, SLOTS), F32)
@@ -138,20 +142,22 @@
             src_ref=statics.at[0],
             dst_ref=statics.at[slot],
             send_sem=static_send,
-            recv_sem=static_recv.at[(slot - 1) // 2],
+            recv_sem=static_recv.at[(slot + 1) // 4],
             device_id=device,
             device_id_type=MESH,
         )
 
-    def moment_group(slot):
-        return 0 if slot < 5 else slot // 9 + (1 if slot < 9 else 1)
+    def stage(slot):
+        if slot < 9:
+            return 0 if slot < 3 else (1 if slot < 5 else 2)
+        return 2 * (slot // 9) + (1 if slot % 9 < 5 else 2)
 
     def moment_copy(turn, slot, device):
         return pltpu.make_async_remote_copy(
             src_ref=moments.at[turn, 0],
             dst_ref=moments.at[turn, slot],
             send_sem=moment_send.at[turn],
-            recv_sem=moment_recv.at[turn, moment_group(slot)],
+            recv_sem=moment_recv.at[turn, stage(slot)],
             device_id=device,
             device_id_type=MESH,
         )
@@ -162,18 +168,32 @@
     for k in range(26, 0, -1):
         static_copy(mirror[k], peers[k]).start()
 
-    def fill(k, buffer):
-        for at in range(6):
+    high, rest = split(jnp.concatenate([-screening * root, -root], axis=0))
+    low = rest.astype(BF16)
+    goal_pairs = jnp.concatenate([high, low, high, low, jnp.zeros((8, SLOTS), BF16)], axis=0)
+
+    def fill(k, buffer, damping):
+        def pairs_of():
+            high, rest = split(statics[k, 4:6])
+            low = rest.astype(BF16)
+            pairs = jnp.concatenate([high, high, low, low, jnp.zeros((8, SLOTS), BF16)], axis=0)
+            damping[...] = lax.dot_general(
+                pairs, goal_pairs, (((0,), (0,)), ((), ())), preferred_element_type=F32
+            ).reshape(GROUPS, 8, SLOTS)
+
+        def column_of(at):
             buffer[at] = columns(places[k, at : at + 1] if at < 3 else statics[k, at : at + 1])
-        buffer[6] = columns(statics[k, 6:7])
+
+        return [pairs_of] + [functools.partial(column_of, at) for at in range(4)]
 
     def spread(row, half):
         return jnp.broadcast_to(row[:, half * 128 : half * 128 + 128], (8, 128))
 
-    def geometry(k, buffer, own):
-        sums = [None] * 6
+    def geometry(k, buffer, damping, weights, own, between=()):
+        between = list(between)
         for half in range(2):
-            goal = [spread(row, half) for row in place + [-root, screening, label]]
+            lanes = pl.ds(half * 128, 128)
+            goal = [spread(row, half) for row in place + [label]]
             for c in range(GROUPS // CHUNK):
                 at = pl.ds(c * CHUNK, CHUNK)
                 deltas = [goal[d] - buffer[d, at] for d in range(3)]
@@ -187,59 +207,76 @@
                 inside = jnp.maximum(1.0 - dist_sq, 0.0)
                 inverse_sq = inverse * inverse
                 radial = (inside * inside) * inverse * inverse_sq
-                cubed = dist_sq * dist_sq * inverse
-                power = (goal[4] + buffer[4, at]) * (goal[3] * buffer[3, at]) * cubed
+                power = damping[at, :, lanes] * (dist_sq * dist_sq * inverse)
                 decay = jnp.exp2(power)
                 three = 1.0 - decay
                 five = three + (power * LN2) * decay
                 direct = radial * three
-                coef_b[k, at, :, pl.ds(half * 128, 128)] = direct
-                coef_a[k, at, :, pl.ds(half * 128, 128)] = radial * inverse_sq * five
-                weight = jnp.where(goal[5] != buffer[5, at], direct * buffer[6, at], 0.0)
-                for d in range(3):
-                    term = jnp.sum(weight * deltas[d], axis=0)
-                    old = sums[3 * half + d]
-                    sums[3 * half + d] = term if old is None else old + term
-        for half in range(2):
-            for d in range(3):
-                lanes = pl.ds(half * 128, 128)
-                if own:
-                    totals[d, :, lanes] = sums[3 * half + d]
-                else:
-                    totals[d, :, lanes] += sums[3 * half + d]
+                coef_b[k, at, :, lanes] = direct
+                coef_a[k, at, :, lanes] = radial * inverse_sq * five
+                weight = jnp.where(goal[3] != buffer[3, at], direct, 0.0)
+                high, rest = split(weight.reshape(CHUNK * 8, 128))
+                weights[0, pl.ds(c * CHUNK * 8, CHUNK * 8), lanes] = high
+                weights[1, pl.ds(c * CHUNK * 8, CHUNK * 8), lanes] = rest.astype(BF16)
+                if between:
+                    between.pop(0)()
+
+    def charges(k, weights):
+        charge_row = statics[k, 6:7]
+        rows = [charge_row] + [charge_row * places[k, d : d + 1] for d in range(3)]
+        high, rest = split(jnp.concatenate(rows + [jnp.zeros((12, SLOTS), F32)], axis=0))
+        middle, rest = split(rest)
+        left = jnp.concatenate([high, middle, rest.astype(BF16)], axis=0)
+        part = jnp.dot(left, weights[0], preferred_element_type=F32)
+        part += jnp.dot(left, weights[1], preferred_element_type=F32)
+        sums_a[...] += part
 
     def arrive(k):
-        for d, step in enumerate((lax.rem(k, 3), lax.rem(k // 3, 3), k // 9)):
-            moved = code_offset(step).astype(F32) * SCALE
+        at = lax.rem(k, 9)
+        sign = jnp.where(lax.rem(at, 2) == 1, SCALE, -SCALE)
+        middle = jnp.logical_and(at > 2, at < 5)
+        x = jnp.where(jnp.logical_or(at == 0, middle), 0.0, sign)
+        y = jnp.where(at < 3, 0.0, jnp.where(at < 7, sign, -sign))
+        z = code_offset(k // 9).astype(F32) * SCALE
+        for d, moved in enumerate((x, y, z)):
             places[k, d : d + 1] = statics[k, d : d + 1] + moved
 
-    fill(0, even)
-    geometry(0, even, True)
-
-    def wait_pair(p):
-        landed(statics.at[pl.ds(2 * p + 1, 2)], static_recv.at[p])
-        arrive(2 * p + 1)
-        arrive(2 * p + 2)
-
-    wait_pair(jnp.int32(0))
-    fill(1, odd)
-
-    def box_pair(p, carry):
-        k = 2 * p + 1
-        fill(k + 1, even)
-        geometry(k, odd, False)
-
-        @pl.when(p < 12)
-        def _():
-            wait_pair(p + 1)
-
-        fill(jnp.minimum(k + 2, 26), odd)
-        geometry(k + 1, even, False)
+    for piece in fill(0, even, even_damping):
+        piece()
+    geometry(0, even, even_damping, even_weights, True)
+    sums_a[...] = jnp.zeros_like(sums_a)
+
+    def run_block(boxes):
+        pending = functools.partial(charges, boxes[0] - 1, even_weights)
+        held = ((odd, odd_damping, odd_weights), (even, even_damping, even_weights))
+        for piece in fill(boxes[0], odd, odd_damping):
+            piece()
+        for at, k in enumerate(boxes):
+            buffer, damping, weights = held[at % 2]
+            between = []
+            if at + 1 < len(boxes):
+                between = fill(boxes[at + 1], *held[(at + 1) % 2][:2])
+            geometry(k, buffer, damping, weights, False, between + [pending])
+            pending = functools.partial(charges, k, weights)
+
+    landed(statics.at[pl.ds(1, 2)], static_recv.at[0])
+    for k in (1, 2):
+        arrive(jnp.int32(k))
+    run_block([1, 2])
+
+    def box_quad(q, carry):
+        base = 4 * q + 3
+        landed(statics.at[pl.ds(base, 4)], static_recv.at[q + 1])
+        for at in range(4):
+            arrive(base + at)
+        run_block([base + at for at in range(4)])
         return carry
 
-    lax.fori_loop(0, 13, box_pair, 0)
-
-    permanent = [jnp.sum(totals[d], axis=0, keepdims=True) for d in range(3)]
+    lax.fori_loop(0, 6, box_quad, 0)
+    charges(26, even_weights)
+    tall = sums_a[...]
+    tall = tall[0:16] + tall[16:32] + tall[32:48]
+    permanent = [place[d] * tall[0:1] - tall[1 + d : 2 + d] for d in range(3)]
     to_shift = jnp.where(live, DRUDE_GAIN * drude, 0.0)
     to_moment = to_shift * drude * (1.0 / CUTOFF**3)
 
@@ -310,13 +347,17 @@
         def _():
             choose()
 
-        landed(moments.at[turn, pl.ds(1, 4)], moment_recv.at[turn, 0])
-        induced(turn, [1, 2, 3, 4], False)
-        landed(moments.at[turn, pl.ds(5, 4)], moment_recv.at[turn, 1])
+        landed(moments.at[turn, pl.ds(1, 2)], moment_recv.at[turn, 0])
+        induced(turn, [1, 2], False)
+        landed(moments.at[turn, pl.ds(3, 2)], moment_recv.at[turn, 1])
+        induced(turn, [3, 4], False)
+        landed(moments.at[turn, pl.ds(5, 4)], moment_recv.at[turn, 2])
         induced(turn, [5, 6, 7, 8], False)
         for side in (near, 3 - near):
-            landed(moments.at[turn, pl.ds(side * 9, 9)], moment_recv.at[turn, side + 1])
-            induced(turn, [side * 9 + at for at in range(9)], False)
+            landed(moments.at[turn, pl.ds(side * 9, 5)], moment_recv.at[turn, 2 * side + 1])
+            induced(turn, [side * 9 + at for at in range(5)], False)
+            landed(moments.at[turn, pl.ds(side * 9 + 5, 4)], moment_recv.at[turn, 2 * side + 2])
+            induced(turn, [side * 9 + at for at in range(5, 9)], False)
         landed(moments.at[turn, pl.ds(1, 26)], moment_send.at[turn])
         tall, wide = sums_a[...], sums_b[...]
         tall = tall[0:16] + tall[16:32] + tall[32:48]
@@ -408,11 +449,14 @@
             pltpu.VMEM((27, 8, SLOTS), F32),
             pltpu.VMEM((27, 4, SLOTS), F32),
             pltpu.VMEM((ITERS, 27, 4, SLOTS), F32),
-            pltpu.VMEM((7, GROUPS, 8, 128), F32),
-            pltpu.VMEM((7, GROUPS, 8, 128), F32),
+            pltpu.VMEM((4, GROUPS, 8, 128), F32),
+            pltpu.VMEM((4, GROUPS, 8, 128), F32),
+            pltpu.VMEM((GROUPS, 8, SLOTS), F32),
+            pltpu.VMEM((GROUPS, 8, SLOTS), F32),
+            pltpu.VMEM((2, SLOTS, SLOTS), BF16),
+            pltpu.VMEM((2, SLOTS, SLOTS), BF16),
             pltpu.VMEM((27, GROUPS, 8, SLOTS), F32),
             pltpu.VMEM((27, GROUPS, 8, SLOTS), F32),
-            pltpu.VMEM((3, 8, SLOTS), F32),
             pltpu.VMEM((48, SLOTS), F32),
             pltpu.VMEM((48, SLOTS), F32),
             pltpu.VMEM((SLOTS + 8, 128), F32),
@@ -421,9 +465,9 @@
             pltpu.VMEM((6, 16, 128), F32),
             pltpu.SemaphoreType.DMA((9,)),
             pltpu.SemaphoreType.DMA,
-            pltpu.SemaphoreType.DMA((13,)),
+            pltpu.SemaphoreType.DMA((7,)),
             pltpu.SemaphoreType.DMA((ITERS,)),
-            pltpu.SemaphoreType.DMA((ITERS, 4)),
+            pltpu.SemaphoreType.DMA((ITERS, 7)),
             pltpu.SemaphoreType.DMA,
             pltpu.SemaphoreType.DMA,
         ],

time: 56.2 us -> 53.3 us (0.948)
  Pallas kernels: 52.8 us -> 49.9 us
    pallas_call x1, Pallas kernels: 52.8 us -> 49.9 us  [local(): call(fractions.reshape(3, 1, SLOTS), velocity.reshape(3, 1, SLOTS), *flat...]
where the time goes in v2:
time: 53.3 us; the launch traced here: 53.1 us
  Pallas kernels  49.9 us (94%)
  local copies, waits for them, and re-layouts  1.9 us (4%)
  between operations  1.3 us (2%)
    pallas_call x1, Pallas kernels, local(): call(fractions.reshape(3, 1, SLOTS), velocity.reshape(3, 1, SLOTS), *flat...  49.9 us
    unnamed x4, local copies, waits for them, and re-layouts  1.9 us

profile of v2, /device:TPU:1, one launch (start us, length us, event | category | flops | bytes accessed | tf_op | source)
XLA Modules:
  0.0 53.1 jit_solution(12944410478660764952)
XLA Ops:
  1.3 49.9 %shard_map.104 = (f32[9,1,256]{2,1,0:T(1,128)}, f32[14,1,96]{2,1,0:T(1,128)}) custom-call(f32[3,1,256]{2,1,0:T(1,128)} %bitcast.16, f32[3,1,256]{2,1,0:T(1,128)} %bitcast.17, f32[1,1,256]{2,1,0:T(1,128)} %bitcast.19, f32[1,1,256]{2,1,0:T(1,128)} %bitcast.20, f32[1,1,256]{2,1,0:T(1,128)} %bitcast.21, s32[1,1,256]{2,1,0:T(1,128)} %bitcast.22, ...), custom_call_target="tpu_custom_call" | custom-call | tf_op jit(solution)/shard_map/pallas_call | solution.py:481
  51.2 0.0 copy-start
  51.2 1.3 %copy.16 = f32[1,1,1,9,256]{4,2,3,1,0:T(1,128)} copy(f32[1,1,1,9,256]{4,2,3,1,0:T(1,128)} %bitcast.14) | data formatting | bytes 18432
  52.5 0.0 copy-done
  52.5 0.6 %copy.17 = f32[1,1,1,14,96]{4,2,3,1,0:T(1,128)} copy(f32[1,1,1,14,96]{4,2,3,1,0:T(1,128)S(1)} %bitcast.15) | data formatting | bytes 10752
Async XLA Ops:
  51.2 1.3 %copy-start = (f32[14,1,96]{2,1,0:T(1,128)S(1)}, f32[14,1,96]{2,1,0:T(1,128)}, u32[]{:S(2)}) copy-start(f32[14,1,96]{2,1,0:T(1,128)} %get-tuple-element.5) | copy-start | bytes 16132
